TPU v7x, 32 devices: a whole 2x2x4 slice. The times are simulated.
32 devices in a mesh: chan: 16 (over z, x, core), facet: 2 (over y).
Axes of the slice: x: 2, y: 2, z: 4, core: 2. Of those that a mesh axis runs over, the one named last changes fastest.
Arguments:
- gradients: bfloat16 [64, 4, 1024, 1024], P('chan', None, 'facet'), may hold values from -6 to 6
- taper_map: float32 [1024, 1024], P('facet'), may hold values from 0.1 to 1
- freq_basis: bfloat16 [64, 4], replicated, may hold values from -0.75 to 0.75
- mixing: float32 [4, 4], replicated, may hold values from -3 to 3
- term_model: float32 [16, 1024, 1024], P('chan', 'facet'), may hold values from -6 to 6
Outputs:
- chan_model: bfloat16 [64, 4, 1024, 1024], P('chan', None, 'facet')
- updated: float32 [16, 1024, 1024], P('chan', 'facet')
All inputs are finite; a program needn't handle non-finite values.
Results may differ from a plain program's by a relative error of at most 0.0071.
Values may be sent and summed in bfloat16 or wider, within the bound.
A program may use at most 192 MiB of HBM per device.

v0:
```python
import jax
import jax.numpy as jnp
from jax import lax
from jax.sharding import PartitionSpec as P

step_size = 0.3
smooth_weight = 0.2
threshold = 0.5


def extended(cells, sides, width):
    for axis, dim in sides:
        count = lax.axis_size(axis)
        ends = count - 1
        head = lax.slice_in_dim(cells, 0, width, axis=dim)
        tail = lax.slice_in_dim(cells, cells.shape[dim] - width, cells.shape[dim], axis=dim)
        cells = jnp.concatenate(
            [
                lax.ppermute(tail, axis, [(i, (i + 1) % count) for i in range(ends)]),
                cells,
                lax.ppermute(head, axis, [((i + 1) % count, i) for i in range(ends)]),
            ],
            axis=dim,
        )
    return cells


def laplace(current):
    padded = extended(current.astype(jnp.bfloat16), (("facet", 1),), 1).astype(current.dtype)
    vertical = padded[:, 2:, :] + padded[:, :-2, :]
    widened = jnp.pad(current, ((0, 0), (0, 0), (1, 1)))
    lateral = widened[:, :, 2:] + widened[:, :, :-2]
    return 4.0 * current - vertical - lateral


def on_device(gradients, taper_map, freq_basis, mixing, term_model):
    local_chans = gradients.shape[0]
    facets = gradients.shape[1]
    band_rows = gradients.shape[2]
    columns = gradients.shape[3]
    term_count = freq_basis.shape[1]
    group_index = lax.axis_index("chan")
    own_basis = lax.dynamic_slice_in_dim(freq_basis, group_index * local_chans, local_chans, 0)
    contracted = jnp.einsum(
        "ks,kfrc->sfrc", own_basis, gradients, preferred_element_type=jnp.float32
    )
    driving = jnp.einsum("ts,sfrc->tfrc", mixing, contracted, precision=lax.Precision.HIGHEST)
    driving_flat = driving.reshape(term_count * facets, band_rows, columns)
    summed = lax.psum_scatter(driving_flat, "chan", scatter_dimension=0, tiled=True)
    stepped = term_model + step_size * (taper_map * summed - smooth_weight * laplace(term_model))
    updated = stepped - jnp.clip(stepped, -threshold, threshold)
    rounded = updated.astype(jnp.bfloat16)
    all_slabs = lax.all_gather(rounded, "chan", axis=0, tiled=True)
    term_images = all_slabs.reshape(term_count, facets, band_rows, columns)
    summed_model = jnp.einsum(
        "kt,tfrc->kfrc", own_basis, term_images, preferred_element_type=jnp.float32
    )
    chan_model = (taper_map * summed_model).astype(jnp.bfloat16)
    return (chan_model, updated)


def solution(mesh):
    return jax.shard_map(
        on_device,
        mesh=mesh,
        in_specs=(
            P("chan", None, "facet", None),
            P("facet", None),
            P(),
            P(),
            P("chan", "facet", None),
        ),
        out_specs=(P("chan", None, "facet", None), P("chan", "facet", None)),
        check_vma=False,
    )
```

profile of v0, /device:TPU:0, one launch (start us, length us, event | category | flops | bytes accessed | tf_op | source)
XLA Modules:
  0.0 653.6 jit_solution(18023688174978968484)
XLA Ops:
  7.2 0.0 copy-start
  7.2 0.0 reduce-scatter.2.cloned.1.call-start
  7.2 43.1 %fusion.1 = f32[4,4,512,1024]{3,0,2,1:T(4,128)} fusion(bf16[4,4,512,1024]{3,2,1,0:T(8,128)(2,1)} %param.5, bf16[64,4]{0,1:T(4,128)(2,1)} %param.7, s32[]{:T(128)S(6)} %select_n.3), kind=kOutput, calls=%fused_computation.3 | convolution fusion | flops 67108864 | bytes 50332164 | tf_op jit(solution)/shard_map/ks,kfrc->sfrc/dot_general | solution.py:44
  50.4 0.0 copy-done
  50.4 62.8 %convolution_bitcast_fusion = f32[4,4,512,1024]{3,0,2,1:T(4,128)} fusion(f32[4,4,512,1024]{3,0,2,1:T(4,128)} %fusion.1, f32[4,4]{1,0:T(4,128)S(1)} %copy-done), kind=kOutput, calls=%fused_computation.1 | convolution fusion | flops 402653184 | bytes 67108928 | tf_op jit(solution)/shard_map/ts,sfrc->tfrc/dot_general | solution.py:47
  113.2 31.8 %copy.14 = f32[4,4,512,1024]{3,2,1,0:T(8,128)} copy(f32[4,4,512,1024]{3,0,2,1:T(4,128)} %convolution_bitcast_fusion) | data formatting | bytes 67108864 | tf_op jit(solution)/shard_map/ts,sfrc->tfrc/dot_general | solution.py:47
  145.0 0.0 copy-start.2
  145.0 0.0 reduce-scatter.2.cloned.1.call-update
  145.0 0.0 all-gather.2.cloned.1.call-start
  145.1 1.5 copy-done.2
  146.6 0.2 convert_element_type.22
  146.8 4.9 collective-permute-start
  151.7 1.5 collective-permute-start.1
  153.2 0.0 collective-permute-done
  153.2 4.0 collective-permute-done.1
  157.2 0.3 maximum_convert_fusion
  157.5 0.0 copy-start.3
  157.5 321.0 %reduce-scatter.2.cloned.1.call-done = f32[1,512,1024]{2,1,0:T(8,128)} async-done(((f32[16,512,1024]{2,1,0:T(8,128)}), f32[1,512,1024]{2,1,0:T(8,128)}) %reduce-scatter.2.cloned.1.call-update) | async-done | bytes 2097168 | tf_op jit(solution)/shard_map/reduce_scatter | solution.py:49
  478.4 7.3 %fusion.17 = (bf16[1,512,1024]{2,1,0:T(8,128)(2,1)}, f32[1,512,1024]{2,1,0:T(8,128)}) fusion(f32[1,512,1024]{2,1,0:T(8,128)} %param.9, f32[1,514,1024]{2,1,0:T(8,128)S(1)} %maximum_convert_fusion, f32[1,512,1024]{2,1,0:T(8,128)} %reduce-scatter.2.cloned.1.call-done, f32[512,1024]{1,0:T(8,128)} %param.6), kind=kLoop, calls=%fused_computation.25 | loop fusion | flops 6815744 | bytes 13631488 | tf_op jit(solution)/shard_map/convert_element_type | solution.py:52
  485.8 0.0 all-gather.2.cloned.1.call-update
  485.8 125.7 %all-gather.2.cloned.1.call-done = bf16[16,512,1024]{2,1,0:T(8,128)(2,1)} async-done(((bf16[1,512,1024]{2,1,0:T(8,128)(2,1)}), bf16[16,512,1024]{2,1,0:T(8,128)(2,1)}) %all-gather.2.cloned.1.call-update) | async-done | bytes 16777232 | tf_op jit(solution)/shard_map/all_gather | solution.py:53
  611.5 0.0 copy-done.3
  611.5 23.5 %multiply_convert_fusion = bf16[4,4,512,1024]{3,0,2,1:T(4,128)(2,1)S(1)} fusion(bf16[4,4,512,1024]{3,2,1,0:T(8,128)(2,1)} %bitcast.26, f32[512,1024]{1,0:T(8,128)} %param.6, bf16[64,4]{0,1:T(4,128)(2,1)S(1)} %copy-done.3, s32[]{:T(128)S(6)} %select_n.3), kind=kOutput, calls=%fused_computation | convolution fusion | flops 83886080 | bytes 35652100 | tf_op jit(solution)/shard_map/kt,tfrc->kfrc/dot_general | solution.py:55
  635.0 0.0 copy-start.1
  635.0 11.8 %copy.17 = bf16[4,4,512,1024]{3,2,1,0:T(8,128)(2,1)} copy(bf16[4,4,512,1024]{3,0,2,1:T(4,128)(2,1)S(1)} %multiply_convert_fusion) | data formatting | bytes 33554432
  646.8 0.0 copy-done.1
  (1 shorter events, 0.0 us)
Async XLA Ops:
  7.2 43.2 %copy-start = (f32[4,4]{1,0:T(4,128)S(1)}, f32[4,4]{1,0:T(4,128)}, u32[]{:S(2)}) copy-start(f32[4,4]{1,0:T(4,128)} %param.8) | copy-start | bytes 196
  7.2 471.3 %reduce-scatter.2.cloned.1.call-start = ((), (), s32[]{:S(2)}) async-start(), calls=%async_computation.1 | async-start | bytes 35651584 | tf_op jit(solution)/shard_map/reduce_scatter | solution.py:49
  145.0 1.6 copy-start.2
  145.0 466.5 %all-gather.2.cloned.1.call-start = ((), (), s32[]{:S(2)}) async-start(), calls=%async_computation.2 | async-start | bytes 17825792 | tf_op jit(solution)/shard_map/all_gather | solution.py:53
  146.8 6.4 collective-permute-start
  151.7 5.5 collective-permute-start.1
  157.5 454.0 %copy-start.3 = (bf16[64,4]{0,1:T(4,128)(2,1)S(1)}, bf16[64,4]{0,1:T(4,128)(2,1)}, u32[]{:S(2)}) copy-start(bf16[64,4]{0,1:T(4,128)(2,1)} %param.7) | copy-start | bytes 1540
  635.0 11.8 %copy-start.1 = (f32[4,4]{1,0:T(4,128)S(1)}, f32[4,4]{1,0:T(4,128)}, u32[]{:S(2)}) copy-start(f32[4,4]{1,0:T(4,128)} %param.8) | copy-start | bytes 196
Sparse Core Ops, SparseCore 0:
  145.1 333.2 reduce-scatter.1
  485.9 125.5 all-gather.1
where the time goes:
time: 654 us
  waiting for transfers between devices  451 us (69%)
  matrix products  129 us (20%)
  local copies, waits for them, and re-layouts  45.1 us (7%)
  between operations  14.1 us (2%)
  other arithmetic  7.78 us (1%)
    reduce_scatter x1, waiting for transfers between devices, on_device(): lax.psum_scatter(driving_flat, 'chan', scatter_dimension=0, tiled=True)  321 us
    all_gather x1, waiting for transfers between devices, on_device(): all_slabs = lax.all_gather(rounded, 'chan', axis=0, tiled=True)  126 us
    dot_general x1, matrix products, on_device(): jnp.einsum('ts,sfrc->tfrc', mixing, contracted, precision=lax.Precision.H...  62.8 us
    dot_general x1, matrix products, on_device(): jnp.einsum('ks,kfrc->sfrc', own_basis, gradients, preferred_element_type=...  43.1 us
    dot_general x1, local copies, waits for them, and re-layouts, on_device(): jnp.einsum('ts,sfrc->tfrc', mixing, contracted, precision=lax.Precision.H...  31.8 us
    dot_general x1, matrix products, on_device(): jnp.einsum('kt,tfrc->kfrc', own_basis, term_images, preferred_element_typ...  23.5 us
    unnamed x9, local copies, waits for them, and re-layouts  13.3 us
  transfers between devices with their start and end apart: 4, of which 3 were waited for; matrix products, arithmetic and copies ran while one was open for 0% of the time, Pallas kernels for 0%

commit v1 on v0

v1 whole, which is shorter than its diff:
```python
import functools

import jax
import jax.numpy as jnp
from jax import lax
from jax.experimental import pallas as pl
from jax.experimental.pallas import tpu as pltpu
from jax.sharding import PartitionSpec as P

step_size = 0.3
smooth_weight = 0.2
threshold = 0.5
chunks = 2


def extended(cells, axis, dim):
    count = lax.axis_size(axis)
    ends = count - 1
    head = lax.slice_in_dim(cells, 0, 1, axis=dim)
    tail = lax.slice_in_dim(cells, cells.shape[dim] - 1, cells.shape[dim], axis=dim)
    return jnp.concatenate(
        [
            lax.ppermute(tail, axis, [(i, i + 1) for i in range(ends)]),
            cells,
            lax.ppermute(head, axis, [(i + 1, i) for i in range(ends)]),
        ],
        axis=dim,
    )


def laplace(current):
    padded = extended(current.astype(jnp.bfloat16), "facet", 1).astype(current.dtype)
    vertical = padded[:, 2:, :] + padded[:, :-2, :]
    widened = jnp.pad(current, ((0, 0), (0, 0), (1, 1)))
    lateral = widened[:, :, 2:] + widened[:, :, :-2]
    return 4.0 * current - vertical - lateral


def divisor(size, most):
    best = 1
    for candidate in range(1, most + 1):
        if size % candidate == 0:
            best = candidate
    return best


def combine_kernel(tapered, strip, width, weights_ref, images_ref, *refs):
    out_ref = refs[-1]
    outs, ins = out_ref.shape[0], images_ref.shape[0]
    rows, columns = out_ref.shape[2], out_ref.shape[3]

    @pl.loop(0, rows // strip)
    def _(step):
        at = pl.ds(pl.multiple_of(step * strip, strip), strip)
        for left in range(0, columns, width):
            across = pl.ds(left, width)
            cells = [images_ref[i, 0, at, across].astype(jnp.float32) for i in range(ins)]
            taper = refs[0][at, across] if tapered else None
            for o in range(outs):
                total = weights_ref[o, 0] * cells[0]
                for i in range(1, ins):
                    total = total + weights_ref[o, i] * cells[i]
                if tapered:
                    total = total * taper
                out_ref[o, 0, at, across] = total.astype(out_ref.dtype)


def combine(weights, images, taper, out_rows, first_in, first_out, rows, earlier):
    outs, ins = weights.shape
    facets, columns = images.shape[1], images.shape[3]
    tile = divisor(rows, 128)
    strip = divisor(tile, 16)
    width = divisor(columns, 512)
    in_tile, out_tile = first_in // tile, first_out // tile
    operands = [weights, images]
    specs = [
        pl.BlockSpec(memory_space=pltpu.SMEM),
        pl.BlockSpec((ins, 1, tile, columns), lambda r, f: (0, f, in_tile + r, 0)),
    ]
    if taper is not None:
        operands.append(taper)
        specs.append(pl.BlockSpec((tile, columns), lambda r, f: (out_tile + r, 0)))
    aliases = {}
    if earlier is not None:
        aliases = {len(operands): 0}
        operands.append(earlier)
        specs.append(pl.BlockSpec(memory_space=pl.ANY))
    pixels = facets * rows * columns
    return pl.pallas_call(
        functools.partial(combine_kernel, taper is not None, strip, width),
        out_shape=jax.ShapeDtypeStruct((outs, facets, out_rows, columns), jnp.bfloat16),
        grid=(rows // tile, facets),
        in_specs=specs,
        out_specs=pl.BlockSpec((outs, 1, tile, columns), lambda r, f: (0, f, out_tile + r, 0)),
        input_output_aliases=aliases,
        cost_estimate=pl.CostEstimate(
            flops=2 * outs * ins * pixels, bytes_accessed=2 * (outs + ins) * pixels, transcendentals=0
        ),
    )(*operands)


def on_device(gradients, taper_map, freq_basis, mixing, term_model):
    local_chans, facets, band_rows, columns = gradients.shape
    term_count = freq_basis.shape[1]
    own_basis = lax.dynamic_slice_in_dim(
        freq_basis, lax.axis_index("chan") * local_chans, local_chans, 0
    ).astype(jnp.float32)
    weights = jnp.sum(mixing[:, None, :] * own_basis[None, :, :], axis=2)
    smoothed = term_model - (step_size * smooth_weight) * laplace(term_model)
    rows = band_rows // chunks
    summed = []
    for chunk in range(chunks):
        driving = combine(weights, gradients, None, rows, chunk * rows, 0, rows, None)
        flat = driving.reshape(term_count * facets, rows, columns)
        summed.append(lax.psum_scatter(flat, "chan", scatter_dimension=0, tiled=True))
    pieces = []
    chan_model = None
    for chunk in range(chunks):
        at = chunk * rows
        taper = taper_map[at : at + rows]
        stepped = smoothed[:, at : at + rows] + step_size * (
            taper * summed[chunk].astype(jnp.float32)
        )
        updated = stepped - jnp.clip(stepped, -threshold, threshold)
        pieces.append(updated)
        slabs = lax.all_gather(updated.astype(jnp.bfloat16), "chan", axis=0, tiled=True)
        terms = slabs.reshape(term_count, facets, rows, columns)
        chan_model = combine(own_basis, terms, taper_map, band_rows, 0, at, rows, chan_model)
    updated = pieces[0] if chunks == 1 else jnp.concatenate(pieces, axis=1)
    return (chan_model, updated)


def solution(mesh):
    return jax.shard_map(
        on_device,
        mesh=mesh,
        in_specs=(
            P("chan", None, "facet", None),
            P("facet", None),
            P(),
            P(),
            P("chan", "facet", None),
        ),
        out_specs=(P("chan", None, "facet", None), P("chan", "facet", None)),
        check_vma=False,
    )
```

time: 654 us -> 405 us (0.62)
  matrix products: 129 us -> 0 us
  waiting for transfers between devices: 451 us -> 326 us
  Pallas kernels: 0 us -> 43.7 us
  local copies, waits for them, and re-layouts: 45.1 us -> 2.55 us
    reduce_scatter x1 -> x2, waiting for transfers between devices: 321 us -> 187 us  [on_device(): lax.psum_scatter(flat, 'chan', scatter_dimension=0, tiled=True)]
    dot_general x3 -> x0, matrix products: 129 us -> none  [the longest x1 62.8 us: on_device(): jnp.einsum('ts,sfrc->tfrc', mixing, contracted, precision=lax.Precision.H...]
    pallas_call x0 -> x4, Pallas kernels: none -> 43.7 us  [combine(): pl.pallas_call(functools.partial(combine_kernel, taper is not None, strip...]
    dot_general x1 -> x0, local copies, waits for them, and re-layouts: 31.8 us -> none  [on_device(): jnp.einsum('ts,sfrc->tfrc', mixing, contracted, precision=lax.Precision.H...]
    unnamed x9 -> x13, local copies, waits for them, and re-layouts: 13.3 us -> 2.46 us
    all_gather x1 -> x2, waiting for transfers between devices: 126 us -> 134 us  [on_device(): lax.all_gather(updated.astype(jnp.bfloat16), 'chan', axis=0, tiled=True)]
  transfers between devices with their start and end apart: 4 -> 6, of which waited for: 3 -> 5; matrix products, arithmetic and copies ran while one was open for 0% -> 1% of each run, Pallas kernels for 0% -> 5%
where the time goes in v1:
time: 405 us; the launch traced here: 404 us
  waiting for transfers between devices  326 us (80%)
  Pallas kernels  43.7 us (11%)
  between operations  13.8 us (3%)
  other arithmetic  10.7 us (3%)
  starting transfers between devices  6.6 us (2%)
    reduce_scatter x2, waiting for transfers between devices, on_device(): lax.psum_scatter(flat, 'chan', scatter_dimension=0, tiled=True)  187 us
    all_gather x2, waiting for transfers between devices, on_device(): lax.all_gather(updated.astype(jnp.bfloat16), 'chan', axis=0, tiled=True)  134 us
    pallas_call x4, Pallas kernels, combine(): pl.pallas_call(functools.partial(combine_kernel, taper is not None, strip...  43.7 us
  transfers between devices with their start and end apart: 6, of which 5 were waited for; matrix products, arithmetic and copies ran while one was open for 1% of the time, Pallas kernels for 5%

profile of v1, /device:TPU:0, one launch (start us, length us, event | category | flops | bytes accessed | tf_op | source)
XLA Modules:
  0.0 403.7 jit_solution(4634560107415696462)
XLA Ops:
  7.2 0.0 copy-start
  7.2 0.0 reduce-scatter.5.cloned.1.call-start
  7.2 0.6 copy-done
  7.9 0.1 constant_dynamic-slice_fusion
  7.9 0.1 copy.11
  8.0 0.0 copy-start.5
  8.0 1.3 multiply_reduce_fusion.weights_ref
  9.4 10.5 %shard_map.69 = bf16[4,4,256,1024]{3,2,1,0:T(8,128)(2,1)} custom-call(f32[4,4]{1,0:T(4,128)} %multiply_reduce_fusion.weights_ref, bf16[4,4,512,1024]{3,2,1,0:T(8,128)(2,1)} %images_ref.3), custom_call_target="tpu_custom_call" | custom-call | flops 33554432 | bytes 16777216 | tf_op jit(solution)/shard_map/pallas_call | solution.py:89
  19.9 0.0 copy-done.5
  19.9 0.0 reduce-scatter.5.cloned.1.call-update
  20.0 0.0 reduce-scatter.3.cloned.1.call-start
  20.0 10.7 %shard_map.68 = bf16[4,4,256,1024]{3,2,1,0:T(8,128)(2,1)} custom-call(f32[4,4]{1,0:T(4,128)} %multiply_reduce_fusion.weights_ref, bf16[4,4,512,1024]{3,2,1,0:T(8,128)(2,1)} %images_ref.3), custom_call_target="tpu_custom_call" | custom-call | flops 33554432 | bytes 16777216 | tf_op jit(solution)/shard_map/pallas_call | solution.py:89
  30.7 0.0 copy-start.3
  30.7 0.0 reduce-scatter.3.cloned.1.call-update
  30.8 0.0 all-gather.5.cloned.1.call-start
  30.8 1.7 copy-done.3
  32.5 0.2 convert_element_type.32
  32.7 0.0 copy-start.4
  32.7 5.1 %collective-permute-start = (bf16[1,1,1024]{2,1,0:T(2,128)(2,1)S(1)}, bf16[1,1,1024]{2,1,0:T(2,128)(2,1)S(1)}, u32[]{:S(2)}, u32[]{:S(2)}) collective-permute-start(bf16[1,1,1024]{2,1,0:T(2,128)(2,1)S(1)} %get-tuple-element.8), channel_id=1, source_target_pairs={{0,1},{2,3},{4,5},{6,7},{8,9},{10,11},{12,13},{14,15},{16,17},{18,... | collective-permute-start | bytes 6152 | tf_op jit(solution)/shard_map/ppermute | solution.py:23
  37.9 1.3 collective-permute-start.1
  39.2 0.0 collective-permute-done
  39.2 4.2 %collective-permute-done.1 = bf16[1,1,1024]{2,1,0:T(2,128)(2,1)S(1)} collective-permute-done((bf16[1,1,1024]{2,1,0:T(2,128)(2,1)S(1)}, bf16[1,1,1024]{2,1,0:T(2,128)(2,1)S(1)}, u32[]{:S(2)}, u32[]{:S(2)}) %collective-permute-start.1) | collective-permute-done | bytes 2080 | tf_op jit(solution)/shard_map/ppermute | solution.py:25
  43.4 0.3 maximum_convert_fusion
  43.7 0.0 copy-done.4
  43.7 0.0 copy-start.2
  43.7 2.5 fusion.3
  46.2 80.1 %reduce-scatter.5.cloned.1.call-done = bf16[1,256,1024]{2,1,0:T(8,128)(2,1)} async-done(((bf16[16,256,1024]{2,1,0:T(8,128)(2,1)}), bf16[1,256,1024]{2,1,0:T(8,128)(2,1)}) %reduce-scatter.5.cloned.1.call-update) | async-done | bytes 524304 | tf_op jit(solution)/shard_map/reduce_scatter | solution.py:115
  126.3 107.2 %reduce-scatter.3.cloned.1.call-done = bf16[1,256,1024]{2,1,0:T(8,128)(2,1)} async-done(((bf16[16,256,1024]{2,1,0:T(8,128)(2,1)}), bf16[1,256,1024]{2,1,0:T(8,128)(2,1)}) %reduce-scatter.3.cloned.1.call-update) | async-done | bytes 524304 | tf_op jit(solution)/shard_map/reduce_scatter | solution.py:115
  233.5 0.0 copy-done.2
  233.5 3.5 fusion.7
  237.0 0.0 all-gather.5.cloned.1.call-update
  237.0 0.0 all-gather.3.cloned.1.call-start
  237.0 0.5 all-gather.3.cloned.1.call-update
  237.6 2.9 pad_maximum_fusion
  240.5 70.6 %all-gather.5.cloned.1.call-done = bf16[16,256,1024]{2,1,0:T(8,128)(2,1)} async-done(((bf16[1,256,1024]{2,1,0:T(8,128)(2,1)}), bf16[16,256,1024]{2,1,0:T(8,128)(2,1)}) %all-gather.5.cloned.1.call-update) | async-done | bytes 8388624 | tf_op jit(solution)/shard_map/all_gather | solution.py:126
  311.1 11.2 %shard_map.70.refs_1_ = bf16[4,4,512,1024]{3,2,1,0:T(8,128)(2,1)} custom-call(f32[4,4]{1,0:T(4,128)} %copy-done.5, bf16[4,4,256,1024]{3,2,1,0:T(8,128)(2,1)} %bitcast.20, f32[512,1024]{1,0:T(8,128)} %refs_0_.3), custom_call_target="tpu_custom_call" | custom-call | flops 33554432 | bytes 16777216 | tf_op jit(solution)/shard_map/pallas_call | solution.py:89
  322.3 63.7 %all-gather.3.cloned.1.call-done = bf16[16,256,1024]{2,1,0:T(8,128)(2,1)} async-done(((bf16[1,256,1024]{2,1,0:T(8,128)(2,1)}), bf16[16,256,1024]{2,1,0:T(8,128)(2,1)}) %all-gather.3.cloned.1.call-update) | async-done | bytes 8388624 | tf_op jit(solution)/shard_map/all_gather | solution.py:126
  386.0 0.0 copy-start.1
  386.0 11.2 %shard_map.71 = bf16[4,4,512,1024]{3,2,1,0:T(8,128)(2,1)} custom-call(f32[4,4]{1,0:T(4,128)} %copy-done.5, bf16[4,4,256,1024]{3,2,1,0:T(8,128)(2,1)} %bitcast.21, f32[512,1024]{1,0:T(8,128)} %refs_0_.3, bf16[4,4,512,1024]{3,2,1,0:T(8,128)(2,1)} %shard_map.70.refs_1_), custom_call_target="tpu_custom_call", output_to_operand_aliasing={{}: (3, {})} | custom-call | flops 33554432 | bytes 16777216 | tf_op jit(solution)/shard_map/pallas_call | solution.py:89
  397.2 0.0 copy-done.1
  (2 shorter events, 0.0 us)
Async XLA Ops:
  7.2 0.7 copy-start
  7.2 119.1 %reduce-scatter.5.cloned.1.call-start = ((), (), s32[]{:S(2)}) async-start(), calls=%async_computation.4 | async-start | bytes 8912896 | tf_op jit(solution)/shard_map/reduce_scatter | solution.py:115
  8.0 11.9 %copy-start.5 = (f32[4,4]{1,0:T(4,128)}, f32[4,4]{1,0:T(4,128)S(1)}, u32[]{:S(2)}) copy-start(f32[4,4]{1,0:T(4,128)S(1)} %convert_element_type.31.weights_ref) | copy-start | bytes 196
  20.0 213.5 %reduce-scatter.3.cloned.1.call-start = ((), (), s32[]{:S(2)}) async-start(), calls=%async_computation.2 | async-start | bytes 8912896 | tf_op jit(solution)/shard_map/reduce_scatter | solution.py:115
  30.7 1.8 copy-start.3
  30.8 280.3 %all-gather.5.cloned.1.call-start = ((), (), s32[]{:S(2)}) async-start(), calls=%async_computation.5 | async-start | bytes 8912896 | tf_op jit(solution)/shard_map/all_gather | solution.py:126
  32.7 11.0 %copy-start.4 = (f32[1,512,1024]{2,1,0:T(8,128)S(1)}, f32[1,512,1024]{2,1,0:T(8,128)}, u32[]{:S(2)}) copy-start(f32[1,512,1024]{2,1,0:T(8,128)} %param.9) | copy-start | bytes 6291460
  32.7 6.5 %collective-permute-start = (bf16[1,1,1024]{2,1,0:T(2,128)(2,1)S(1)}, bf16[1,1,1024]{2,1,0:T(2,128)(2,1)S(1)}, u32[]{:S(2)}, u32[]{:S(2)}) collective-permute-start(bf16[1,1,1024]{2,1,0:T(2,128)(2,1)S(1)} %get-tuple-element.8), channel_id=1, source_target_pairs={{0,1},{2,3},{4,5},{6,7},{8,9},{10,11},{12,13},{14,15},{16,17},{18,... | collective-permute-start | bytes 6152 | tf_op jit(solution)/shard_map/ppermute | solution.py:23
  37.9 5.5 %collective-permute-start.1 = (bf16[1,1,1024]{2,1,0:T(2,128)(2,1)S(1)}, bf16[1,1,1024]{2,1,0:T(2,128)(2,1)S(1)}, u32[]{:S(2)}, u32[]{:S(2)}) collective-permute-start(bf16[1,1,1024]{2,1,0:T(2,128)(2,1)S(1)} %get-tuple-element.9), channel_id=1, source_target_pairs={{1,0},{3,2},{5,4},{7,6},{9,8},{11,10},{13,12},{15,14},{17,16},{19,... | collective-permute-start | bytes 6152 | tf_op jit(solution)/shard_map/ppermute | solution.py:25
  43.7 189.8 %copy-start.2 = (f32[512,1024]{1,0:T(8,128)S(1)}, f32[512,1024]{1,0:T(8,128)}, u32[]{:S(2)}) copy-start(f32[512,1024]{1,0:T(8,128)} %refs_0_.3) | copy-start | bytes 6291460
  237.0 149.0 %all-gather.3.cloned.1.call-start = ((), (), s32[]{:S(2)}) async-start(), calls=%async_computation.3 | async-start | bytes 8912896 | tf_op jit(solution)/shard_map/all_gather | solution.py:126
  386.0 11.2 %copy-start.1 = (bf16[64,4]{0,1:T(4,128)(2,1)S(1)}, bf16[64,4]{0,1:T(4,128)(2,1)}, u32[]{:S(2)}) copy-start(bf16[64,4]{0,1:T(4,128)(2,1)} %param.7) | copy-start | bytes 1540
Sparse Core Ops, SparseCore 0:
  20.1 106.1 reduce-scatter.4
  130.4 103.0 reduce-scatter.2
  237.1 73.9 all-gather.4
  313.1 72.8 all-gather.2
